TPU v7x, 32 devices: a whole 2x2x4 slice. The times are simulated.
32 devices in a mesh: dp: 8 (over y, x, core), mp: 4 (over z).
Axes of the slice: x: 2, y: 2, z: 4, core: 2. Of those that a mesh axis runs over, the one named last changes fastest.
Arguments:
- hidden_in: bfloat16 [2, 32, 4096], P(None, 'dp', 'mp'), may hold values from -6 to 6
- rec_gain: float32 [2, 4096], replicated, may hold values from 0.5 to 1.5
- rec_in_x: bfloat16 [2, 4096, 4096], P(None, 'dp', 'mp'), may hold values from -0.09375 to 0.09375
- rec_in_y: bfloat16 [2, 4096, 4096], P(None, 'dp', 'mp'), may hold values from -0.09375 to 0.09375
- conv_weight: float32 [2, 4, 4096], P(None, None, 'mp'), may hold values from -3 to 3
- conv_bias: float32 [2, 4096], P(None, 'mp'), may hold values from -3 to 3
- gate_x_weight: bfloat16 [2, 16, 256, 256], P(None, 'mp'), may hold values from -0.375 to 0.375
- gate_x_bias: float32 [2, 4096], P(None, 'mp'), may hold values from -4 to 4
- gate_a_weight: bfloat16 [2, 16, 256, 256], P(None, 'mp'), may hold values from -0.375 to 0.375
- gate_a_bias: float32 [2, 4096], P(None, 'mp'), may hold values from -4 to 4
- decay_param: float32 [2, 4096], P(None, 'mp'), may hold values from -9 to -1
- rec_out: bfloat16 [2, 4096, 4096], P(None, 'dp', 'mp'), may hold values from -0.09375 to 0.09375
- lru_state: bfloat16 [2, 32, 4096], P(None, 'dp', 'mp'), may hold values from -6 to 6
- conv_state: bfloat16 [2, 3, 32, 4096], P(None, None, 'dp', 'mp'), may hold values from -6 to 6
- scale_index: int32 [2], replicated, may hold values from 0 to 7
- attn_gain: float32 [4096], replicated, may hold values from 0.5 to 1.5
- attn_q: bfloat16 [4096, 4096], P('dp', 'mp'), may hold values from -0.09375 to 0.09375
- attn_kv: bfloat16 [4096, 512], P('dp', 'mp'), may hold values from -0.09375 to 0.09375
- attn_out: bfloat16 [4096, 4096], P('dp', 'mp'), may hold values from -0.09375 to 0.09375
- key_cache: bfloat16 [32, 2048, 256], P('dp', 'mp'), may hold values from -400 to 400
- value_cache: bfloat16 [32, 2048, 256], P('dp', 'mp'), may hold values from -6 to 6
- positions: int32 [32], P('dp'), may hold values from 1 to 6143
Outputs:
- hidden_out: bfloat16 [2, 32, 4096], P(None, 'dp', 'mp')
- lru_out: bfloat16 [2, 32, 4096], P(None, 'dp', 'mp')
- conv_out: bfloat16 [2, 3, 32, 4096], P(None, None, 'dp', 'mp')
- new_kv: bfloat16 [2, 32, 512], P(None, 'dp', 'mp')
Inputs may be any that keep to these rules, and one draw needn't show every extreme that they name: `positions`: the count of tokens a sequence has seen; the cache holds its last min(that count, 2048) tokens.
All inputs are finite; a program needn't handle non-finite values.
Results may differ from a plain program's by a relative error of at most 0.03.
Values may be sent and summed in bfloat16 or wider, within the bound.
A program may use at most 64 MiB of HBM per device.

v0:
```python
import jax
import jax.numpy as jnp
from jax import lax
from jax.sharding import PartitionSpec as P

HEADS = 16
HEAD_DIM = 256
WIN = 2048
LAYERS = 2
STEPS = 2


def joined(array, axis, join):
    gathered = jax.tree.map(
        lambda a, kind: lax.all_gather(a.astype(kind), axis),
        array,
        (jnp.bfloat16, jnp.bfloat16, jnp.bfloat16),
    )

    def take(source):
        return jax.tree.map(
            lambda a, own: lax.dynamic_index_in_dim(a, source, 0, False).astype(own.dtype),
            gathered,
            array,
        )

    return lax.fori_loop(
        1, lax.axis_size(axis), lambda source, state: join(state, take(source)), take(0)
    )


def norm_rows(values, gain):
    mean_sq = jnp.mean(values * values, axis=-1, keepdims=True)
    return (values * lax.rsqrt(mean_sq + 1e-06) * gain).astype(jnp.bfloat16)


def spread_project(normed, weight):
    spread = lax.all_to_all(normed, "dp", split_axis=1, concat_axis=0, tiled=True)
    return lax.psum_scatter(
        jnp.dot(spread, weight, preferred_element_type=jnp.float32),
        "dp",
        scatter_dimension=0,
        tiled=True,
    )


def full_stream(stream):
    return lax.all_gather(stream, "mp", axis=1, tiled=True)


def full_features(values):
    return lax.all_gather(values, "mp", axis=1, tiled=True)


def lru_gate(filtered_half, weight, bias):
    rows = filtered_half.shape[0]
    shaped = filtered_half.reshape(rows, weight.shape[0], weight.shape[1])
    mixed = jnp.einsum("bhi,hij->bhj", shaped, weight, preferred_element_type=jnp.float32)
    return jax.nn.sigmoid(mixed.reshape(rows, -1) + bias)


def combine(first, second):
    top_first, total_first, summed_first = first
    top_second, total_second, summed_second = second
    best = jnp.maximum(top_first, top_second)
    fade_first = jnp.exp(top_first - best)
    fade_second = jnp.exp(top_second - best)
    total = total_first * fade_first + total_second * fade_second
    summed = summed_first * fade_first[..., None] + summed_second * fade_second[..., None]
    return (best, total, summed)


def recurrent_layer(
    stream,
    gain,
    in_x,
    in_y,
    conv_taps,
    conv_shift,
    gx_weight,
    gx_bias,
    ga_weight,
    ga_bias,
    decay,
    out_weight,
    state,
    window,
):
    normed = norm_rows(full_stream(stream), gain)
    width = in_x.shape[1]
    both = spread_project(normed, jnp.concatenate([in_x, in_y], axis=1))
    branch_input = both[:, :width]
    branch_gate = both[:, width:]
    driven = branch_input.astype(jnp.bfloat16)
    gating = jax.nn.gelu(branch_gate, approximate=True)
    taps = jnp.concatenate([window, driven[None]], 0)
    filtered = jnp.sum(taps.astype(jnp.float32) * conv_taps[:, None, :], axis=0) + conv_shift
    filtered_half = filtered.astype(jnp.bfloat16)
    input_gate = lru_gate(filtered_half, gx_weight, gx_bias)
    decay_gate = lru_gate(filtered_half, ga_weight, ga_bias)
    log_decay = -8.0 * decay_gate * jax.nn.softplus(decay)
    state = jnp.exp(log_decay) * state + jnp.sqrt(1.0 - jnp.exp(2.0 * log_decay)) * (
        input_gate * filtered
    )
    mixed = (state * gating).astype(jnp.bfloat16)
    stream = stream + spread_project(full_features(mixed), out_weight)
    return (stream, state, taps[1:])


def attention_layer(
    stream,
    gain,
    w_query,
    w_keyvalue,
    w_out,
    key_cache,
    value_cache,
    positions,
    fresh_keys,
    fresh_values,
    step,
):
    normed = norm_rows(full_stream(stream), gain)
    query_cols = w_query.shape[1]
    local = spread_project(normed, jnp.concatenate([w_query, w_keyvalue], axis=1)).astype(
        jnp.bfloat16
    )
    kv_local = local[:, query_cols:]
    rows = local.shape[0]
    groups = full_features(local).reshape(rows, -1, local.shape[1])
    query = groups[:, :, :query_cols].reshape(rows, HEADS, HEAD_DIM)
    key_value = groups[:, :, query_cols:].reshape(rows, 2 * HEAD_DIM)
    fresh_keys.append(key_value[:, :HEAD_DIM])
    fresh_values.append(key_value[:, HEAD_DIM:])
    slots = key_cache.shape[1]
    slot_ids = lax.axis_index("mp") * slots + jnp.arange(slots, dtype=jnp.int32)
    position = positions[:, None]
    held = position - 1 - jnp.mod(position - 1 - slot_ids[None, :], WIN)
    valid = ((held >= 0) & (held >= position + step - WIN + 1))[:, None, :]
    scores = jnp.einsum(
        "bhd,bsd->bhs", query, key_cache, preferred_element_type=jnp.float32
    ) * HEAD_DIM ** (-0.5)
    masked = jnp.where(valid, scores, -1e30)
    top = jnp.max(masked, axis=-1)
    weights = jnp.where(valid, jnp.exp(masked - top[..., None]), 0.0)
    total = jnp.sum(weights, axis=-1)
    summed = jnp.einsum(
        "bhs,bsd->bhd",
        weights.astype(jnp.bfloat16),
        value_cache,
        preferred_element_type=jnp.float32,
    )
    top, total, summed = joined((top, total, summed), "mp", combine)
    new_keys = jnp.stack(fresh_keys, 1)
    new_values = jnp.stack(fresh_values, 1)
    fresh_scores = jnp.einsum(
        "bhd,bnd->bhn", query, new_keys, preferred_element_type=jnp.float32
    ) * HEAD_DIM ** (-0.5)
    best = jnp.maximum(top, jnp.max(fresh_scores, axis=-1))
    fade = jnp.exp(top - best)
    fresh_weights = jnp.exp(fresh_scores - best[..., None])
    total = total * fade + jnp.sum(fresh_weights, axis=-1)
    summed = summed * fade[..., None] + jnp.einsum(
        "bhn,bnd->bhd",
        fresh_weights.astype(jnp.bfloat16),
        new_values,
        preferred_element_type=jnp.float32,
    )
    attended = (summed / total[..., None]).astype(jnp.bfloat16).reshape(rows, HEADS * HEAD_DIM)
    stream = stream + spread_project(attended, w_out)
    return (stream, kv_local)


def body(
    hidden_in,
    rec_gain,
    rec_in_x,
    rec_in_y,
    conv_weight,
    conv_bias,
    gate_x_weight,
    gate_x_bias,
    gate_a_weight,
    gate_a_bias,
    decay_param,
    rec_out,
    lru_state,
    conv_state,
    scale_index,
    attn_gain,
    attn_q,
    attn_kv,
    attn_out,
    key_cache,
    value_cache,
    positions,
):
    scales = 2.0 ** ((scale_index.astype(jnp.float32) - 4.0) * 0.5)
    states = [lru_state[layer].astype(jnp.float32) * scales[layer] for layer in range(LAYERS)]
    windows = [conv_state[layer] for layer in range(LAYERS)]
    fresh_keys = []
    fresh_values = []
    outputs = []
    kv_parts = []
    for step in range(STEPS):
        stream = hidden_in[step].astype(jnp.float32)
        for layer in range(LAYERS):
            stream, states[layer], windows[layer] = recurrent_layer(
                stream,
                rec_gain[layer],
                rec_in_x[layer],
                rec_in_y[layer],
                conv_weight[layer],
                conv_bias[layer],
                gate_x_weight[layer],
                gate_x_bias[layer],
                gate_a_weight[layer],
                gate_a_bias[layer],
                decay_param[layer],
                rec_out[layer],
                states[layer],
                windows[layer],
            )
        stream, kv_local = attention_layer(
            stream,
            attn_gain,
            attn_q,
            attn_kv,
            attn_out,
            key_cache,
            value_cache,
            positions,
            fresh_keys,
            fresh_values,
            step,
        )
        kv_parts.append(kv_local)
        outputs.append(stream.astype(jnp.bfloat16))
    lru_new = jnp.stack(
        [(states[layer] / scales[layer]).astype(jnp.bfloat16) for layer in range(LAYERS)], 0
    )
    return (jnp.stack(outputs, 0), lru_new, jnp.stack(windows, 0), jnp.stack(kv_parts, 0))


def solution(mesh):
    placed = (
        P(None, "dp", "mp"),
        P(),
        P(None, "dp", "mp"),
        P(None, "dp", "mp"),
        P(None, None, "mp"),
        P(None, "mp"),
        P(None, "mp", None, None),
        P(None, "mp"),
        P(None, "mp", None, None),
        P(None, "mp"),
        P(None, "mp"),
        P(None, "dp", "mp"),
        P(None, "dp", "mp"),
        P(None, None, "dp", "mp"),
        P(),
        P(),
        P("dp", "mp"),
        P("dp", "mp"),
        P("dp", "mp"),
        P("dp", "mp", None),
        P("dp", "mp", None),
        P("dp"),
    )
    return jax.shard_map(
        body,
        mesh=mesh,
        in_specs=placed,
        out_specs=(
            P(None, "dp", "mp"),
            P(None, "dp", "mp"),
            P(None, None, "dp", "mp"),
            P(None, "dp", "mp"),
        ),
        check_vma=False,
    )
```

profile of v0, /device:TPU:0, one launch (start us, length us, event | category | flops | bytes accessed | tf_op | source)
XLA Modules:
  0.0 668.5 jit_solution(16265052284147277069)
XLA Ops:
  8.0 14.9 %all-gather.4 = f32[1,4,4096]{2,1,0:T(4,128)S(1)} all-gather(f32[1,4,1024]{2,1,0:T(4,128)S(1)} %get-tuple-element.445), channel_id=6, replica_groups=mesh['dp'=8,'mp'=4] {'mp'}, dimensions={2}, use_global_device_ids=true | all-gather | bytes 81920 | tf_op jit(solution)/shard_map/all_gather | solution.py:48
  23.1 13.3 %all-gather = f32[1,4,4096]{2,1,0:T(4,128)S(1)} all-gather(f32[1,4,1024]{2,1,0:T(4,128)S(1)} %get-tuple-element.444), channel_id=2, replica_groups=mesh['dp'=8,'mp'=4] {'mp'}, dimensions={2}, use_global_device_ids=true | all-gather | bytes 81920 | tf_op jit(solution)/shard_map/all_gather | solution.py:48
  47.4 4.2 slice_bitcast_fusion
  52.2 4.2 all-to-all-start.6
  56.5 4.8 all-to-all-done.6
  65.6 52.1 %all-reduce.33.cloned.1.call-done = (f32[32,2048]{1,0:T(8,128)}, f32[32,2048]{1,0:T(8,128)}) async-done(((f32[32,2048]{1,0:T(8,128)}, f32[32,2048]{1,0:T(8,128)}), (f32[32,2048]{1,0:T(8,128)}, f32[32,2048]{1,0:T(8,128)})) %all-reduce.33.cloned.1.call-update) | async-done | bytes 524304
  126.6 13.8 %all_gather.75 = bf16[4,4096]{1,0:T(4,128)(2,1)} all-gather(bf16[4,1024]{1,0:T(4,128)(2,1)S(1)} %fusion.125), channel_id=1, replica_groups=mesh['dp'=8,'mp'=4] {'mp'}, dimensions={1}, use_global_device_ids=true | all-gather | bytes 40960 | tf_op jit(solution)/shard_map/all_gather | solution.py:52
  143.8 13.8 %all_gather.65 = bf16[4,4096]{1,0:T(4,128)(2,1)} all-gather(bf16[4,1024]{1,0:T(4,128)(2,1)S(1)} %get-tuple-element.424), channel_id=1, replica_groups=mesh['dp'=8,'mp'=4] {'mp'}, dimensions={1}, use_global_device_ids=true | all-gather | bytes 40960 | tf_op jit(solution)/shard_map/all_gather | solution.py:52
  161.8 4.8 all-to-all-done.1
  169.2 52.6 %all-reduce.31.cloned.1.call-done = (f32[32,1024]{1,0:T(8,128)}, f32[32,1024]{1,0:T(8,128)}) async-done(((f32[32,1024]{1,0:T(8,128)}, f32[32,1024]{1,0:T(8,128)}), (f32[32,1024]{1,0:T(8,128)}, f32[32,1024]{1,0:T(8,128)})) %all-reduce.31.cloned.1.call-update) | async-done | bytes 262160
  222.6 13.2 %all_gather.76 = f32[4,4096]{1,0:T(4,128)S(1)} all-gather(f32[4,1024]{1,0:T(4,128)S(1)} %get-tuple-element.441), channel_id=1, replica_groups=mesh['dp'=8,'mp'=4] {'mp'}, dimensions={1}, use_global_device_ids=true | all-gather | bytes 81920 | tf_op jit(solution)/shard_map/all_gather | solution.py:48
  235.9 13.2 %all_gather.66 = f32[4,4096]{1,0:T(4,128)S(1)} all-gather(f32[4,1024]{1,0:T(4,128)S(1)} %get-tuple-element.440), channel_id=1, replica_groups=mesh['dp'=8,'mp'=4] {'mp'}, dimensions={1}, use_global_device_ids=true | all-gather | bytes 81920 | tf_op jit(solution)/shard_map/all_gather | solution.py:48
  272.2 52.5 %all-reduce.29.cloned.1.call-done = (f32[32,2048]{1,0:T(8,128)}, f32[32,2048]{1,0:T(8,128)}) async-done(((f32[32,2048]{1,0:T(8,128)}, f32[32,2048]{1,0:T(8,128)}), (f32[32,2048]{1,0:T(8,128)}, f32[32,2048]{1,0:T(8,128)})) %all-reduce.29.cloned.1.call-update) | async-done | bytes 524304
  331.6 13.9 %all_gather.77 = bf16[4,4096]{1,0:T(4,128)(2,1)} all-gather(bf16[4,1024]{1,0:T(4,128)(2,1)S(1)} %fusion.124), channel_id=1, replica_groups=mesh['dp'=8,'mp'=4] {'mp'}, dimensions={1}, use_global_device_ids=true | all-gather | bytes 40960 | tf_op jit(solution)/shard_map/all_gather | solution.py:52
  349.5 13.9 %all_gather.67 = bf16[4,4096]{1,0:T(4,128)(2,1)} all-gather(bf16[4,1024]{1,0:T(4,128)(2,1)S(1)} %get-tuple-element.422), channel_id=1, replica_groups=mesh['dp'=8,'mp'=4] {'mp'}, dimensions={1}, use_global_device_ids=true | all-gather | bytes 40960 | tf_op jit(solution)/shard_map/all_gather | solution.py:52
  375.2 52.5 %all-reduce.27.cloned.1.call-done = (f32[32,1024]{1,0:T(8,128)}, f32[32,1024]{1,0:T(8,128)}) async-done(((f32[32,1024]{1,0:T(8,128)}, f32[32,1024]{1,0:T(8,128)}), (f32[32,1024]{1,0:T(8,128)}, f32[32,1024]{1,0:T(8,128)})) %all-reduce.27.cloned.1.call-update) | async-done | bytes 262160
  428.5 13.2 %all_gather.68 = f32[4,4096]{1,0:T(4,128)S(1)} all-gather(f32[4,1024]{1,0:T(4,128)S(1)} %dynamic-slice_add_fusion.4), channel_id=1, replica_groups=mesh['dp'=8,'mp'=4] {'mp'}, dimensions={1}, use_global_device_ids=true | all-gather | bytes 81920 | tf_op jit(solution)/shard_map/all_gather | solution.py:48
  442.7 13.2 %all_gather.78 = f32[4,4096]{1,0:T(4,128)S(1)} all-gather(f32[4,1024]{1,0:T(4,128)S(1)} %dynamic-slice_add_fusion.1), channel_id=1, replica_groups=mesh['dp'=8,'mp'=4] {'mp'}, dimensions={1}, use_global_device_ids=true | all-gather | bytes 81920 | tf_op jit(solution)/shard_map/all_gather | solution.py:48
  460.7 4.2 all-to-all-done.4
  468.5 4.4 all-to-all-done.10
  473.9 25.9 %all-reduce.34 = (bf16[32,1152]{1,0:T(8,128)(2,1)S(1)}, bf16[32,1152]{1,0:T(8,128)(2,1)S(1)}) all-reduce(f32[32,1152]{1,0:T(8,128)} %fusion.177, f32[32,1152]{1,0:T(8,128)S(1)} %fusion.175), channel_id=20, replica_groups=mesh['dp'=8,'mp'=4] {'dp'}, use_global_device_ids=true, to_apply=%region_24.25.clone | all-reduce | flops 73728 | bytes 442368
  499.8 13.2 %all_gather.69 = bf16[4,4608]{1,0:T(4,128)(2,1)S(1)} all-gather(bf16[4,1152]{1,0:T(4,128)(2,1)S(1)} %dynamic-slice_convert_fusion.1), channel_id=1, replica_groups=mesh['dp'=8,'mp'=4] {'mp'}, dimensions={1}, use_global_device_ids=true | all-gather | bytes 46080 | tf_op jit(solution)/shard_map/all_gather | solution.py:52
  513.1 13.2 %all_gather.79 = bf16[4,4608]{1,0:T(4,128)(2,1)S(1)} all-gather(bf16[4,1152]{1,0:T(4,128)(2,1)S(1)} %dynamic-slice_convert_fusion), channel_id=1, replica_groups=mesh['dp'=8,'mp'=4] {'mp'}, dimensions={1}, use_global_device_ids=true | all-gather | bytes 46080 | tf_op jit(solution)/shard_map/all_gather | solution.py:52
  528.5 13.4 %all-gather.3 = bf16[16,16,256]{2,1,0:T(8,128)(2,1)S(1)} all-gather(bf16[4,16,256]{2,1,0:T(8,128)(2,1)S(1)} %convolution_convert_fusion.1), channel_id=5, replica_groups=mesh['dp'=8,'mp'=4] {'mp'}, dimensions={0}, use_global_device_ids=true | all-gather | bytes 163840 | tf_op jit(solution)/shard_map/all_gather | solution.py:15
  541.9 10.8 %all-gather.9 = bf16[4,4,16]{2,1,0:T(4,128)(2,1)S(1)} all-gather(bf16[1,4,16]{2,1,0:T(4,128)(2,1)S(1)} %bitcast.382), channel_id=4, replica_groups=mesh['dp'=8,'mp'=4] {'mp'}, dimensions={0}, use_global_device_ids=true | all-gather | bytes 640 | tf_op jit(solution)/shard_map/all_gather | solution.py:15
  552.7 7.6 %all-gather.8 = bf16[4,4,16]{2,1,0:T(4,128)(2,1)S(1)} all-gather(bf16[1,4,16]{2,1,0:T(4,128)(2,1)S(1)} %convert_bitcast_fusion.3), channel_id=3, replica_groups=mesh['dp'=8,'mp'=4] {'mp'}, dimensions={0}, use_global_device_ids=true | all-gather | bytes 640 | tf_op jit(solution)/shard_map/all_gather | solution.py:15
  564.8 13.4 %all-gather.7 = bf16[16,16,256]{2,1,0:T(8,128)(2,1)S(1)} all-gather(bf16[4,16,256]{2,1,0:T(8,128)(2,1)S(1)} %convolution_convert_fusion), channel_id=9, replica_groups=mesh['dp'=8,'mp'=4] {'mp'}, dimensions={0}, use_global_device_ids=true | all-gather | bytes 163840 | tf_op jit(solution)/shard_map/all_gather | solution.py:15
  578.2 9.6 %all-gather.11 = bf16[4,4,16]{2,1,0:T(4,128)(2,1)S(1)} all-gather(bf16[1,4,16]{2,1,0:T(4,128)(2,1)S(1)} %bitcast.381), channel_id=8, replica_groups=mesh['dp'=8,'mp'=4] {'mp'}, dimensions={0}, use_global_device_ids=true | all-gather | bytes 640 | tf_op jit(solution)/shard_map/all_gather | solution.py:15
  587.8 7.6 %all-gather.10 = bf16[4,4,16]{2,1,0:T(4,128)(2,1)S(1)} all-gather(bf16[1,4,16]{2,1,0:T(4,128)(2,1)S(1)} %convert_bitcast_fusion.1), channel_id=7, replica_groups=mesh['dp'=8,'mp'=4] {'mp'}, dimensions={0}, use_global_device_ids=true | all-gather | bytes 640 | tf_op jit(solution)/shard_map/all_gather | solution.py:15
  596.9 4.2 all-to-all-start.11
  601.2 4.8 all-to-all-done.11
  608.5 51.3 %all-reduce.25.cloned.1.call-done = (f32[32,1024]{1,0:T(8,128)}, f32[32,1024]{1,0:T(8,128)}) async-done(((f32[32,1024]{1,0:T(8,128)}, f32[32,1024]{1,0:T(8,128)}), (f32[32,1024]{1,0:T(8,128)}, f32[32,1024]{1,0:T(8,128)})) %all-reduce.25.cloned.1.call-update) | async-done | bytes 262160
  (237 shorter events, 106.6 us)
Async XLA Ops:
  7.2 519.2 %copy-start = (bf16[4,512,256]{2,1,0:T(8,128)(2,1)S(1)}, bf16[4,512,256]{2,1,0:T(8,128)(2,1)}, u32[]{:S(2)}) copy-start(bf16[4,512,256]{2,1,0:T(8,128)(2,1)} %param.45) | copy-start | bytes 3145732
  38.1 14.1 %all-to-all-start = ((bf16[4,8,512]{2,0,1:T(4,128)(2,1)}), bf16[4,8,512]{2,0,1:T(4,128)(2,1)S(1)}, u32[]{:S(2)}, u32[]{:S(2)}) async-start(bf16[4,8,512]{2,0,1:T(4,128)(2,1)} %bitcast.12), calls=%async_computation | async-start | bytes 65536 | tf_op jit(solution)/shard_map/all_to_all | solution.py:38
  44.6 81.1 %copy-start.14 = (f32[1,1024]{1,0:T(1,128)}, f32[1,1024]{1,0:T(1,128)S(1)}, u32[]{:S(2)}) copy-start(f32[1,1024]{1,0:T(1,128)S(1)} %get-tuple-element.453) | copy-start | bytes 12292
  46.0 79.8 %copy-start.16 = (f32[1,1024]{1,0:T(1,128)}, f32[1,1024]{1,0:T(1,128)S(1)}, u32[]{:S(2)}) copy-start(f32[1,1024]{1,0:T(1,128)S(1)} %get-tuple-element.447) | copy-start | bytes 12292
  47.4 78.4 %copy-start.18 = (f32[1,1024]{1,0:T(1,128)}, f32[1,1024]{1,0:T(1,128)S(1)}, u32[]{:S(2)}) copy-start(f32[1,1024]{1,0:T(1,128)S(1)} %get-tuple-element.449) | copy-start | bytes 12292
  52.2 73.5 %copy-start.20 = (f32[1,1024]{1,0:T(1,128)}, f32[1,1024]{1,0:T(1,128)S(1)}, u32[]{:S(2)}) copy-start(f32[1,1024]{1,0:T(1,128)S(1)} %get-tuple-element.451) | copy-start | bytes 12292
  52.2 9.0 %all-to-all-start.6 = ((bf16[4,8,512]{2,0,1:T(4,128)(2,1)}), bf16[4,8,512]{2,0,1:T(4,128)(2,1)S(1)}, u32[]{:S(2)}, u32[]{:S(2)}) async-start(bf16[4,8,512]{2,0,1:T(4,128)(2,1)} %bitcast.72), calls=%async_computation.6 | async-start | bytes 65536 | tf_op jit(solution)/shard_map/all_to_all | solution.py:38
  56.4 61.3 %all-reduce.33.cloned.1.call-start = ((), (), s32[]{:S(2)}) async-start(), calls=%async_computation.16 | async-start | bytes 1048576
  63.6 60.6 %copy-start.8 = (bf16[2,4,1024]{2,1,0:T(4,128)(2,1)S(1)}, bf16[2,4,1024]{2,1,0:T(4,128)(2,1)}, u32[]{:S(2)}) copy-start(bf16[2,4,1024]{2,1,0:T(4,128)(2,1)} %param.38) | copy-start | bytes 49156
  63.6 80.2 %copy-start.27 = (s32[4]{0:T(128)S(1)}, s32[4]{0:T(128)}, u32[]{:S(2)}) copy-start(s32[4]{0:T(128)} %param.47) | copy-start | bytes 52
  63.6 103.0 %copy-start.1 = (bf16[2,512,1024]{2,1,0:T(8,128)(2,1)S(1)}, bf16[2,512,1024]{2,1,0:T(8,128)(2,1)}, u32[]{:S(2)}) copy-start(bf16[2,512,1024]{2,1,0:T(8,128)(2,1)} %param.37) | copy-start | bytes 6291460
  121.8 100.0 %copy-start.9 = (bf16[2,4,1024]{2,1,0:T(4,128)(2,1)S(1)}, bf16[2,4,1024]{2,1,0:T(4,128)(2,1)}, u32[]{:S(2)}) copy-start(bf16[2,4,1024]{2,1,0:T(4,128)(2,1)} %param.26) | copy-start | bytes 49156
  140.4 17.2 %all-to-all-start.7 = ((bf16[4,8,512]{2,0,1:T(4,128)(2,1)}), bf16[4,8,512]{2,0,1:T(4,128)(2,1)S(1)}, u32[]{:S(2)}, u32[]{:S(2)}) async-start(bf16[4,8,512]{2,0,1:T(4,128)(2,1)} %bitcast.80), calls=%async_computation.7 | async-start | bytes 65536 | tf_op jit(solution)/shard_map/all_to_all | solution.py:38
  157.6 9.0 %all-to-all-start.1 = ((bf16[4,8,512]{2,0,1:T(4,128)(2,1)}), bf16[4,8,512]{2,0,1:T(4,128)(2,1)S(1)}, u32[]{:S(2)}, u32[]{:S(2)}) async-start(bf16[4,8,512]{2,0,1:T(4,128)(2,1)} %bitcast.31), calls=%async_computation.1 | async-start | bytes 65536 | tf_op jit(solution)/shard_map/all_to_all | solution.py:38
  161.8 60.0 %all-reduce.31.cloned.1.call-start = ((), (), s32[]{:S(2)}) async-start(), calls=%async_computation.15 | async-start | bytes 524288
  168.5 98.4 %copy-start.5 = (bf16[512,1024]{1,0:T(8,128)(2,1)S(1)}, bf16[512,1024]{1,0:T(8,128)(2,1)}, u32[]{:S(2)}) copy-start(bf16[512,1024]{1,0:T(8,128)(2,1)} %get-tuple-element.428) | copy-start | bytes 3145732
  250.0 8.1 %all-to-all-start.2 = ((bf16[4,8,512]{2,0,1:T(4,128)(2,1)}), bf16[4,8,512]{2,0,1:T(4,128)(2,1)S(1)}, u32[]{:S(2)}, u32[]{:S(2)}) async-start(bf16[4,8,512]{2,0,1:T(4,128)(2,1)} %bitcast.36), calls=%async_computation.2 | async-start | bytes 65536 | tf_op jit(solution)/shard_map/all_to_all | solution.py:38
  258.1 8.1 %all-to-all-start.8 = ((bf16[4,8,512]{2,0,1:T(4,128)(2,1)}), bf16[4,8,512]{2,0,1:T(4,128)(2,1)S(1)}, u32[]{:S(2)}, u32[]{:S(2)}) async-start(bf16[4,8,512]{2,0,1:T(4,128)(2,1)} %bitcast.82), calls=%async_computation.8 | async-start | bytes 65536 | tf_op jit(solution)/shard_map/all_to_all | solution.py:38
  261.4 63.2 %all-reduce.29.cloned.1.call-start = ((), (), s32[]{:S(2)}) async-start(), calls=%async_computation.14 | async-start | bytes 1048576
  270.7 58.5 %copy-start.13 = (f32[1,1024]{1,0:T(1,128)S(1)}, f32[1,1024]{1,0:T(1,128)}, u32[]{:S(2)}) copy-start(f32[1,1024]{1,0:T(1,128)} %get-tuple-element.450) | copy-start | bytes 12292
  329.1 126.9 %copy-start.25 = (f32[4096]{0:T(1024)S(1)}, f32[4096]{0:T(1024)}, u32[]{:S(2)}) copy-start(f32[4096]{0:T(1024)} %param.41) | copy-start | bytes 49156
  345.4 18.0 %all-to-all-start.9 = ((bf16[4,8,512]{2,0,1:T(4,128)(2,1)}), bf16[4,8,512]{2,0,1:T(4,128)(2,1)S(1)}, u32[]{:S(2)}, u32[]{:S(2)}) async-start(bf16[4,8,512]{2,0,1:T(4,128)(2,1)} %bitcast.90), calls=%async_computation.9 | async-start | bytes 65536 | tf_op jit(solution)/shard_map/all_to_all | solution.py:38
  363.4 9.0 %all-to-all-start.3 = ((bf16[4,8,512]{2,0,1:T(4,128)(2,1)}), bf16[4,8,512]{2,0,1:T(4,128)(2,1)S(1)}, u32[]{:S(2)}, u32[]{:S(2)}) async-start(bf16[4,8,512]{2,0,1:T(4,128)(2,1)} %bitcast.55), calls=%async_computation.3 | async-start | bytes 65536 | tf_op jit(solution)/shard_map/all_to_all | solution.py:38
  367.5 60.3 %all-reduce.27.cloned.1.call-start = ((), (), s32[]{:S(2)}) async-start(), calls=%async_computation.13 | async-start | bytes 524288
  442.7 83.7 %copy-start.23 = (pred[4,512]{1,0:T(4,128)(4,1)S(1)}, pred[4,512]{1,0:T(4,128)(4,1)}, u32[]{:S(2)}) copy-start(pred[4,512]{1,0:T(4,128)(4,1)} %get-tuple-element.463) | copy-start | bytes 6148
  456.7 8.1 %all-to-all-start.4 = ((bf16[4,8,512]{2,0,1:T(4,128)(2,1)}), bf16[4,8,512]{2,0,1:T(4,128)(2,1)S(1)}, u32[]{:S(2)}, u32[]{:S(2)}) async-start(bf16[4,8,512]{2,0,1:T(4,128)(2,1)} %bitcast.58), calls=%async_computation.4 | async-start | bytes 65536 | tf_op jit(solution)/shard_map/all_to_all | solution.py:38
  464.8 8.1 %all-to-all-start.10 = ((bf16[4,8,512]{2,0,1:T(4,128)(2,1)}), bf16[4,8,512]{2,0,1:T(4,128)(2,1)S(1)}, u32[]{:S(2)}, u32[]{:S(2)}) async-start(bf16[4,8,512]{2,0,1:T(4,128)(2,1)} %bitcast.92), calls=%async_computation.10 | async-start | bytes 65536 | tf_op jit(solution)/shard_map/all_to_all | solution.py:38
  468.5 58.5 %copy-start.2 = (bf16[4,512,256]{2,1,0:T(8,128)(2,1)S(1)}, bf16[4,512,256]{2,1,0:T(8,128)(2,1)}, u32[]{:S(2)}) copy-start(bf16[4,512,256]{2,1,0:T(8,128)(2,1)} %param.46) | copy-start | bytes 3145732
  528.1 77.8 %copy-start.3 = (bf16[512,1024]{1,0:T(8,128)(2,1)S(1)}, bf16[512,1024]{1,0:T(8,128)(2,1)}, u32[]{:S(2)}) copy-start(bf16[512,1024]{1,0:T(8,128)(2,1)} %param.44) | copy-start | bytes 3145732
  561.4 35.4 %all-to-all-start.5 = ((bf16[4,8,512]{2,0,1:T(4,128)(2,1)}), bf16[4,8,512]{2,0,1:T(4,128)(2,1)S(1)}, u32[]{:S(2)}, u32[]{:S(2)}) async-start(bf16[4,8,512]{2,0,1:T(4,128)(2,1)} %copy.95), calls=%async_computation.5 | async-start | bytes 65536 | tf_op jit(solution)/shard_map/all_to_all | solution.py:38
  596.9 9.1 %all-to-all-start.11 = ((bf16[4,8,512]{2,0,1:T(4,128)(2,1)}), bf16[4,8,512]{2,0,1:T(4,128)(2,1)S(1)}, u32[]{:S(2)}, u32[]{:S(2)}) async-start(bf16[4,8,512]{2,0,1:T(4,128)(2,1)} %copy.107), calls=%async_computation.11 | async-start | bytes 65536 | tf_op jit(solution)/shard_map/all_to_all | solution.py:38
  601.1 58.7 %all-reduce.25.cloned.1.call-start = ((), (), s32[]{:S(2)}) async-start(), calls=%async_computation.12 | async-start | bytes 524288
  (15 other events, 314.8 us)
Sparse Core Ops, SparseCore 0:
  63.7 53.8 all-reduce.32
  168.6 53.0 all-reduce.30
  270.8 53.8 all-reduce.28
  374.7 53.0 all-reduce.26
  608.0 51.7 all-reduce.24
where the time goes:
time: 671 us; the launch traced here: 669 us
  waiting for transfers between devices  293 us (44%)
  blocking collectives  251 us (37%)
  starting transfers between devices  43.8 us (7%)
  matrix products  25.1 us (4%)
  other arithmetic  20.7 us (3%)
  local copies, waits for them, and re-layouts  20 us (3%)
  between operations  15.2 us (2%)
    unnamed x10, waiting for transfers between devices  261 us
    all_gather x6, blocking collectives, full_features(): return lax.all_gather(values, 'mp', axis=1, tiled=True)  81.7 us
    all_gather x6, blocking collectives, full_stream(): return lax.all_gather(stream, 'mp', axis=1, tiled=True)  81 us
    all_gather x6, blocking collectives, joined(): lax.all_gather(a.astype(kind), axis)  62.3 us
    all_to_all x12, starting transfers between devices, spread_project(): lax.all_to_all(normed, 'dp', split_axis=1, concat_axis=0, tiled=True)  43.7 us
    all_to_all x12, waiting for transfers between devices, spread_project(): lax.all_to_all(normed, 'dp', split_axis=1, concat_axis=0, tiled=True)  31.4 us
    unnamed x1, blocking collectives  25.9 us
    dot_general x12, matrix products, spread_project(): jnp.dot(spread, weight, preferred_element_type=jnp.float32)  15.4 us
  transfers between devices with their start and end apart: 17, of which 13 were waited for; matrix products, arithmetic and copies ran while one was open for 3% of the time, Pallas kernels for 0%

commit v1 on v0

--- a/solution.py
+++ b/solution.py
@@ -35,7 +35,10 @@
 
 
 def spread_project(normed, weight):
-    spread = lax.all_to_all(normed, "dp", split_axis=1, concat_axis=0, tiled=True)
+    spread = jnp.concatenate(
+        lax.all_to_all(jnp.stack(jnp.split(normed, lax.axis_size("dp"), axis=1)), "dp", 0, 0),
+        axis=0,
+    )
     return lax.psum_scatter(
         jnp.dot(spread, weight, preferred_element_type=jnp.float32),
         "dp",

time: 671 us -> 713 us (1.063)
  local copies, waits for them, and re-layouts: 20 us -> 75.4 us
  waiting for transfers between devices: 293 us -> 280 us
    unnamed x66 -> x142, local copies, waits for them, and re-layouts: 2.03 us -> 52 us
    all_to_all x12, waiting for transfers between devices: 31.4 us -> 20.1 us  [spread_project(): lax.all_to_all(jnp.stack(jnp.split(normed, lax.axis_size('dp'), axis=1)),...]
  transfers between devices with their start and end apart: 17 -> 17, of which waited for: 13 -> 11; matrix products, arithmetic and copies ran while one was open for 3% -> 8% of each run, Pallas kernels for 0% -> 0%
where the time goes in v1:
time: 713 us; the launch traced here: 710 us
  waiting for transfers between devices  280 us (39%)
  blocking collectives  248 us (35%)
  local copies, waits for them, and re-layouts  75.4 us (11%)
  starting transfers between devices  45.4 us (6%)
  matrix products  26.6 us (4%)
  other arithmetic  19.4 us (3%)
  between operations  15.1 us (2%)
    unnamed x10, waiting for transfers between devices  260 us
    all_gather x6, blocking collectives, full_stream(): return lax.all_gather(stream, 'mp', axis=1, tiled=True)  81 us
    all_gather x6, blocking collectives, full_features(): return lax.all_gather(values, 'mp', axis=1, tiled=True)  78.8 us
    all_gather x6, blocking collectives, joined(): lax.all_gather(a.astype(kind), axis)  62.3 us
    unnamed x142, local copies, waits for them, and re-layouts  52 us
    all_to_all x12, starting transfers between devices, spread_project(): lax.all_to_all(jnp.stack(jnp.split(normed, lax.axis_size('dp'), axis=1)),...  45.3 us
    unnamed x1, blocking collectives  25.9 us
    all_to_all x12, waiting for transfers between devices, spread_project(): lax.all_to_all(jnp.stack(jnp.split(normed, lax.axis_size('dp'), axis=1)),...  20.1 us
  transfers between devices with their start and end apart: 17, of which 11 were waited for; matrix products, arithmetic and copies ran while one was open for 8% of the time, Pallas kernels for 0%

profile of v1, /device:TPU:0, one launch (start us, length us, event | category | flops | bytes accessed | tf_op | source)
XLA Modules:
  0.0 710.2 jit_solution(11852351363770767202)
XLA Ops:
  8.0 14.9 %all-gather.4 = f32[1,4,4096]{2,1,0:T(4,128)S(1)} all-gather(f32[1,4,1024]{2,1,0:T(4,128)S(1)} %get-tuple-element.445), channel_id=6, replica_groups=mesh['dp'=8,'mp'=4] {'mp'}, dimensions={2}, use_global_device_ids=true | all-gather | bytes 81920 | tf_op jit(solution)/shard_map/all_gather | solution.py:51
  23.1 13.3 %all-gather = f32[1,4,4096]{2,1,0:T(4,128)S(1)} all-gather(f32[1,4,1024]{2,1,0:T(4,128)S(1)} %get-tuple-element.444), channel_id=2, replica_groups=mesh['dp'=8,'mp'=4] {'mp'}, dimensions={2}, use_global_device_ids=true | all-gather | bytes 81920 | tf_op jit(solution)/shard_map/all_gather | solution.py:51
  57.8 4.2 slice_bitcast_fusion
  62.6 4.2 all-to-all-start.6
  74.8 52.2 %all-reduce.33.cloned.1.call-done = (f32[32,2048]{1,0:T(8,128)}, f32[32,2048]{1,0:T(8,128)}) async-done(((f32[32,2048]{1,0:T(8,128)}, f32[32,2048]{1,0:T(8,128)}), (f32[32,2048]{1,0:T(8,128)}, f32[32,2048]{1,0:T(8,128)})) %all-reduce.33.cloned.1.call-update) | async-done | bytes 524304
  135.0 13.1 %all_gather.65 = bf16[4,4096]{1,0:T(4,128)(2,1)S(1)} all-gather(bf16[4,1024]{1,0:T(4,128)(2,1)S(1)} %get-tuple-element.424), channel_id=1, replica_groups=mesh['dp'=8,'mp'=4] {'mp'}, dimensions={1}, use_global_device_ids=true | all-gather | bytes 40960 | tf_op jit(solution)/shard_map/all_gather | solution.py:55
  157.2 13.1 %all_gather.75 = bf16[4,4096]{1,0:T(4,128)(2,1)S(1)} all-gather(bf16[4,1024]{1,0:T(4,128)(2,1)S(1)} %fusion.127), channel_id=1, replica_groups=mesh['dp'=8,'mp'=4] {'mp'}, dimensions={1}, use_global_device_ids=true | all-gather | bytes 40960 | tf_op jit(solution)/shard_map/all_gather | solution.py:55
  175.1 4.1 all-to-all-start.7
  187.3 51.2 %all-reduce.31.cloned.1.call-done = (f32[32,1024]{1,0:T(8,128)}, f32[32,1024]{1,0:T(8,128)}) async-done(((f32[32,1024]{1,0:T(8,128)}, f32[32,1024]{1,0:T(8,128)}), (f32[32,1024]{1,0:T(8,128)}, f32[32,1024]{1,0:T(8,128)})) %all-reduce.31.cloned.1.call-update) | async-done | bytes 262160
  239.3 13.2 %all_gather.76 = f32[4,4096]{1,0:T(4,128)S(1)} all-gather(f32[4,1024]{1,0:T(4,128)S(1)} %get-tuple-element.441), channel_id=1, replica_groups=mesh['dp'=8,'mp'=4] {'mp'}, dimensions={1}, use_global_device_ids=true | all-gather | bytes 81920 | tf_op jit(solution)/shard_map/all_gather | solution.py:51
  252.7 13.2 %all_gather.66 = f32[4,4096]{1,0:T(4,128)S(1)} all-gather(f32[4,1024]{1,0:T(4,128)S(1)} %get-tuple-element.440), channel_id=1, replica_groups=mesh['dp'=8,'mp'=4] {'mp'}, dimensions={1}, use_global_device_ids=true | all-gather | bytes 81920 | tf_op jit(solution)/shard_map/all_gather | solution.py:51
  279.0 4.1 all-to-all-start.8
  292.8 53.1 %all-reduce.29.cloned.1.call-done = (f32[32,2048]{1,0:T(8,128)}, f32[32,2048]{1,0:T(8,128)}) async-done(((f32[32,2048]{1,0:T(8,128)}, f32[32,2048]{1,0:T(8,128)}), (f32[32,2048]{1,0:T(8,128)}, f32[32,2048]{1,0:T(8,128)})) %all-reduce.29.cloned.1.call-update) | async-done | bytes 524304
  351.9 13.1 %all_gather.67 = bf16[4,4096]{1,0:T(4,128)(2,1)S(1)} all-gather(bf16[4,1024]{1,0:T(4,128)(2,1)S(1)} %get-tuple-element.422), channel_id=1, replica_groups=mesh['dp'=8,'mp'=4] {'mp'}, dimensions={1}, use_global_device_ids=true | all-gather | bytes 40960 | tf_op jit(solution)/shard_map/all_gather | solution.py:55
  374.0 13.1 %all_gather.77 = bf16[4,4096]{1,0:T(4,128)(2,1)S(1)} all-gather(bf16[4,1024]{1,0:T(4,128)(2,1)S(1)} %fusion.126), channel_id=1, replica_groups=mesh['dp'=8,'mp'=4] {'mp'}, dimensions={1}, use_global_device_ids=true | all-gather | bytes 40960 | tf_op jit(solution)/shard_map/all_gather | solution.py:55
  392.7 4.1 all-to-all-start.9
  405.2 52.0 %all-reduce.27.cloned.1.call-done = (f32[32,1024]{1,0:T(8,128)}, f32[32,1024]{1,0:T(8,128)}) async-done(((f32[32,1024]{1,0:T(8,128)}, f32[32,1024]{1,0:T(8,128)}), (f32[32,1024]{1,0:T(8,128)}, f32[32,1024]{1,0:T(8,128)})) %all-reduce.27.cloned.1.call-update) | async-done | bytes 262160
  457.9 13.2 %all_gather.68 = f32[4,4096]{1,0:T(4,128)S(1)} all-gather(f32[4,1024]{1,0:T(4,128)S(1)} %dynamic-slice_add_fusion.4), channel_id=1, replica_groups=mesh['dp'=8,'mp'=4] {'mp'}, dimensions={1}, use_global_device_ids=true | all-gather | bytes 81920 | tf_op jit(solution)/shard_map/all_gather | solution.py:51
  472.0 13.2 %all_gather.78 = f32[4,4096]{1,0:T(4,128)S(1)} all-gather(f32[4,1024]{1,0:T(4,128)S(1)} %dynamic-slice_add_fusion.1), channel_id=1, replica_groups=mesh['dp'=8,'mp'=4] {'mp'}, dimensions={1}, use_global_device_ids=true | all-gather | bytes 81920 | tf_op jit(solution)/shard_map/all_gather | solution.py:51
  498.3 4.1 all-to-all-start.10
  502.8 4.5 all-to-all-done.10
  508.3 25.9 %all-reduce.34 = (bf16[32,1152]{1,0:T(8,128)(2,1)S(1)}, bf16[32,1152]{1,0:T(8,128)(2,1)S(1)}) all-reduce(f32[32,1152]{1,0:T(8,128)} %fusion.179, f32[32,1152]{1,0:T(8,128)S(1)} %fusion.177), channel_id=20, replica_groups=mesh['dp'=8,'mp'=4] {'dp'}, use_global_device_ids=true, to_apply=%region_24.25.clone | all-reduce | flops 73728 | bytes 442368
  534.2 13.2 %all_gather.69 = bf16[4,4608]{1,0:T(4,128)(2,1)S(1)} all-gather(bf16[4,1152]{1,0:T(4,128)(2,1)S(1)} %dynamic-slice_convert_fusion.1), channel_id=1, replica_groups=mesh['dp'=8,'mp'=4] {'mp'}, dimensions={1}, use_global_device_ids=true | all-gather | bytes 46080 | tf_op jit(solution)/shard_map/all_gather | solution.py:55
  547.4 13.2 %all_gather.79 = bf16[4,4608]{1,0:T(4,128)(2,1)S(1)} all-gather(bf16[4,1152]{1,0:T(4,128)(2,1)S(1)} %dynamic-slice_convert_fusion), channel_id=1, replica_groups=mesh['dp'=8,'mp'=4] {'mp'}, dimensions={1}, use_global_device_ids=true | all-gather | bytes 46080 | tf_op jit(solution)/shard_map/all_gather | solution.py:55
  562.8 13.4 %all-gather.3 = bf16[16,16,256]{2,1,0:T(8,128)(2,1)S(1)} all-gather(bf16[4,16,256]{2,1,0:T(8,128)(2,1)S(1)} %convolution_convert_fusion.1), channel_id=5, replica_groups=mesh['dp'=8,'mp'=4] {'mp'}, dimensions={0}, use_global_device_ids=true | all-gather | bytes 163840 | tf_op jit(solution)/shard_map/all_gather | solution.py:15
  576.3 10.8 %all-gather.9 = bf16[4,4,16]{2,1,0:T(4,128)(2,1)S(1)} all-gather(bf16[1,4,16]{2,1,0:T(4,128)(2,1)S(1)} %bitcast.754), channel_id=4, replica_groups=mesh['dp'=8,'mp'=4] {'mp'}, dimensions={0}, use_global_device_ids=true | all-gather | bytes 640 | tf_op jit(solution)/shard_map/all_gather | solution.py:15
  587.1 7.6 %all-gather.8 = bf16[4,4,16]{2,1,0:T(4,128)(2,1)S(1)} all-gather(bf16[1,4,16]{2,1,0:T(4,128)(2,1)S(1)} %convert_bitcast_fusion.3), channel_id=3, replica_groups=mesh['dp'=8,'mp'=4] {'mp'}, dimensions={0}, use_global_device_ids=true | all-gather | bytes 640 | tf_op jit(solution)/shard_map/all_gather | solution.py:15
  603.3 13.4 %all-gather.7 = bf16[16,16,256]{2,1,0:T(8,128)(2,1)S(1)} all-gather(bf16[4,16,256]{2,1,0:T(8,128)(2,1)S(1)} %convolution_convert_fusion), channel_id=9, replica_groups=mesh['dp'=8,'mp'=4] {'mp'}, dimensions={0}, use_global_device_ids=true | all-gather | bytes 163840 | tf_op jit(solution)/shard_map/all_gather | solution.py:15
  616.7 9.6 %all-gather.11 = bf16[4,4,16]{2,1,0:T(4,128)(2,1)S(1)} all-gather(bf16[1,4,16]{2,1,0:T(4,128)(2,1)S(1)} %bitcast.753), channel_id=8, replica_groups=mesh['dp'=8,'mp'=4] {'mp'}, dimensions={0}, use_global_device_ids=true | all-gather | bytes 640 | tf_op jit(solution)/shard_map/all_gather | solution.py:15
  626.3 7.6 %all-gather.10 = bf16[4,4,16]{2,1,0:T(4,128)(2,1)S(1)} all-gather(bf16[1,4,16]{2,1,0:T(4,128)(2,1)S(1)} %convert_bitcast_fusion.1), channel_id=7, replica_groups=mesh['dp'=8,'mp'=4] {'mp'}, dimensions={0}, use_global_device_ids=true | all-gather | bytes 640 | tf_op jit(solution)/shard_map/all_gather | solution.py:15
  639.5 4.2 all-to-all-start.11
  650.2 51.3 %all-reduce.25.cloned.1.call-done = (f32[32,1024]{1,0:T(8,128)}, f32[32,1024]{1,0:T(8,128)}) async-done(((f32[32,1024]{1,0:T(8,128)}, f32[32,1024]{1,0:T(8,128)}), (f32[32,1024]{1,0:T(8,128)}, f32[32,1024]{1,0:T(8,128)})) %all-reduce.25.cloned.1.call-update) | async-done | bytes 262160
  (321 shorter events, 154.2 us)
Async XLA Ops:
  7.2 553.5 %copy-start = (bf16[4,512,256]{2,1,0:T(8,128)(2,1)S(1)}, bf16[4,512,256]{2,1,0:T(8,128)(2,1)}, u32[]{:S(2)}) copy-start(bf16[4,512,256]{2,1,0:T(8,128)(2,1)} %param.45) | copy-start | bytes 3145732
  42.3 20.3 %all-to-all-start = ((bf16[8,4,512]{2,1,0:T(4,128)(2,1)}), bf16[8,4,512]{2,1,0:T(4,128)(2,1)S(1)}, u32[]{:S(2)}, u32[]{:S(2)}) async-start(bf16[8,4,512]{2,1,0:T(4,128)(2,1)} %constant_dynamic-update-slice_fusion), calls=%async_computation | async-start | bytes 65536 | tf_op jit(solution)/shard_map/all_to_all | solution.py:39
  52.9 103.3 %copy-start.12 = (f32[1,1024]{1,0:T(1,128)}, f32[1,1024]{1,0:T(1,128)S(1)}, u32[]{:S(2)}) copy-start(f32[1,1024]{1,0:T(1,128)S(1)} %get-tuple-element.453) | copy-start | bytes 12292
  54.3 102.0 %copy-start.14 = (f32[1,1024]{1,0:T(1,128)}, f32[1,1024]{1,0:T(1,128)S(1)}, u32[]{:S(2)}) copy-start(f32[1,1024]{1,0:T(1,128)S(1)} %get-tuple-element.447) | copy-start | bytes 12292
  55.7 100.6 %copy-start.16 = (f32[1,1024]{1,0:T(1,128)}, f32[1,1024]{1,0:T(1,128)S(1)}, u32[]{:S(2)}) copy-start(f32[1,1024]{1,0:T(1,128)S(1)} %get-tuple-element.449) | copy-start | bytes 12292
  57.1 99.2 %copy-start.18 = (f32[1,1024]{1,0:T(1,128)}, f32[1,1024]{1,0:T(1,128)S(1)}, u32[]{:S(2)}) copy-start(f32[1,1024]{1,0:T(1,128)S(1)} %get-tuple-element.451) | copy-start | bytes 12292
  62.6 9.1 %all-to-all-start.6 = ((bf16[8,4,512]{2,1,0:T(4,128)(2,1)}), bf16[8,4,512]{2,1,0:T(4,128)(2,1)S(1)}, u32[]{:S(2)}, u32[]{:S(2)}) async-start(bf16[8,4,512]{2,1,0:T(4,128)(2,1)} %constant_dynamic-update-slice_fusion.50), calls=%async_computation.6 | async-start | bytes 65536 | tf_op jit(solution)/shard_map/all_to_all | solution.py:39
  66.8 60.2 %all-reduce.33.cloned.1.call-start = ((), (), s32[]{:S(2)}) async-start(), calls=%async_computation.16 | async-start | bytes 1048576
  72.9 60.7 %copy-start.6 = (bf16[2,4,1024]{2,1,0:T(4,128)(2,1)S(1)}, bf16[2,4,1024]{2,1,0:T(4,128)(2,1)}, u32[]{:S(2)}) copy-start(bf16[2,4,1024]{2,1,0:T(4,128)(2,1)} %param.38) | copy-start | bytes 49156
  72.9 106.4 %copy-start.1 = (bf16[2,512,1024]{2,1,0:T(8,128)(2,1)S(1)}, bf16[2,512,1024]{2,1,0:T(8,128)(2,1)}, u32[]{:S(2)}) copy-start(bf16[2,512,1024]{2,1,0:T(8,128)(2,1)} %param.37) | copy-start | bytes 6291460
  152.9 22.1 %all-to-all-start.1 = ((bf16[8,4,512]{2,1,0:T(4,128)(2,1)}), bf16[8,4,512]{2,1,0:T(4,128)(2,1)S(1)}, u32[]{:S(2)}, u32[]{:S(2)}) async-start(bf16[8,4,512]{2,1,0:T(4,128)(2,1)} %constant_dynamic-update-slice_fusion.8), calls=%async_computation.1 | async-start | bytes 65536 | tf_op jit(solution)/shard_map/all_to_all | solution.py:39
  175.1 9.0 %all-to-all-start.7 = ((bf16[8,4,512]{2,1,0:T(4,128)(2,1)}), bf16[8,4,512]{2,1,0:T(4,128)(2,1)S(1)}, u32[]{:S(2)}, u32[]{:S(2)}) async-start(bf16[8,4,512]{2,1,0:T(4,128)(2,1)} %constant_dynamic-update-slice_fusion.58), calls=%async_computation.7 | async-start | bytes 65536 | tf_op jit(solution)/shard_map/all_to_all | solution.py:39
  179.2 59.3 %all-reduce.31.cloned.1.call-start = ((), (), s32[]{:S(2)}) async-start(), calls=%async_computation.15 | async-start | bytes 524288
  185.0 98.8 %copy-start.5 = (bf16[512,1024]{1,0:T(8,128)(2,1)S(1)}, bf16[512,1024]{1,0:T(8,128)(2,1)}, u32[]{:S(2)}) copy-start(bf16[512,1024]{1,0:T(8,128)(2,1)} %get-tuple-element.428) | copy-start | bytes 3145732
  270.9 8.1 %all-to-all-start.2 = ((bf16[8,4,512]{2,1,0:T(4,128)(2,1)}), bf16[8,4,512]{2,1,0:T(4,128)(2,1)S(1)}, u32[]{:S(2)}, u32[]{:S(2)}) async-start(bf16[8,4,512]{2,1,0:T(4,128)(2,1)} %constant_dynamic-update-slice_fusion.16), calls=%async_computation.2 | async-start | bytes 65536 | tf_op jit(solution)/shard_map/all_to_all | solution.py:39
  279.0 9.0 %all-to-all-start.8 = ((bf16[8,4,512]{2,1,0:T(4,128)(2,1)}), bf16[8,4,512]{2,1,0:T(4,128)(2,1)S(1)}, u32[]{:S(2)}, u32[]{:S(2)}) async-start(bf16[8,4,512]{2,1,0:T(4,128)(2,1)} %constant_dynamic-update-slice_fusion.66), calls=%async_computation.8 | async-start | bytes 65536 | tf_op jit(solution)/shard_map/all_to_all | solution.py:39
  283.1 62.8 %all-reduce.29.cloned.1.call-start = ((), (), s32[]{:S(2)}) async-start(), calls=%async_computation.14 | async-start | bytes 1048576
  286.2 61.3 %copy-start.8 = (f32[4,1024]{1,0:T(4,128)S(1)}, f32[4,1024]{1,0:T(4,128)}, u32[]{:S(2)}) copy-start(f32[4,1024]{1,0:T(4,128)} %get-tuple-element.432) | copy-start | bytes 49156
  286.2 61.3 %copy-start.4 = (bf16[2,4,256,256]{3,2,1,0:T(8,128)(2,1)S(1)}, bf16[2,4,256,256]{3,2,1,0:T(8,128)(2,1)}, u32[]{:S(2)}) copy-start(bf16[2,4,256,256]{3,2,1,0:T(8,128)(2,1)} %param.34) | copy-start | bytes 3145732
  291.3 59.0 %copy-start.10 = (f32[1,1024]{1,0:T(1,128)S(1)}, f32[1,1024]{1,0:T(1,128)}, u32[]{:S(2)}) copy-start(f32[1,1024]{1,0:T(1,128)} %get-tuple-element.448) | copy-start | bytes 12292
  291.3 59.0 %copy-start.11 = (f32[1,1024]{1,0:T(1,128)S(1)}, f32[1,1024]{1,0:T(1,128)}, u32[]{:S(2)}) copy-start(f32[1,1024]{1,0:T(1,128)} %get-tuple-element.450) | copy-start | bytes 12292
  350.4 135.0 %copy-start.22 = (f32[4096]{0:T(1024)S(1)}, f32[4096]{0:T(1024)}, u32[]{:S(2)}) copy-start(f32[4096]{0:T(1024)} %param.41) | copy-start | bytes 49156
  369.8 22.9 %all-to-all-start.3 = ((bf16[8,4,512]{2,1,0:T(4,128)(2,1)}), bf16[8,4,512]{2,1,0:T(4,128)(2,1)S(1)}, u32[]{:S(2)}, u32[]{:S(2)}) async-start(bf16[8,4,512]{2,1,0:T(4,128)(2,1)} %constant_dynamic-update-slice_fusion.24), calls=%async_computation.3 | async-start | bytes 65536 | tf_op jit(solution)/shard_map/all_to_all | solution.py:39
  392.7 9.0 %all-to-all-start.9 = ((bf16[8,4,512]{2,1,0:T(4,128)(2,1)}), bf16[8,4,512]{2,1,0:T(4,128)(2,1)S(1)}, u32[]{:S(2)}, u32[]{:S(2)}) async-start(bf16[8,4,512]{2,1,0:T(4,128)(2,1)} %constant_dynamic-update-slice_fusion.74), calls=%async_computation.9 | async-start | bytes 65536 | tf_op jit(solution)/shard_map/all_to_all | solution.py:39
  396.9 60.3 %all-reduce.27.cloned.1.call-start = ((), (), s32[]{:S(2)}) async-start(), calls=%async_computation.13 | async-start | bytes 524288
  485.2 75.5 %copy-start.21 = (pred[4,512]{1,0:T(4,128)(4,1)S(1)}, pred[4,512]{1,0:T(4,128)(4,1)}, u32[]{:S(2)}) copy-start(pred[4,512]{1,0:T(4,128)(4,1)} %get-tuple-element.463) | copy-start | bytes 6148
  490.2 8.1 %all-to-all-start.4 = ((bf16[8,4,512]{2,1,0:T(4,128)(2,1)}), bf16[8,4,512]{2,1,0:T(4,128)(2,1)S(1)}, u32[]{:S(2)}, u32[]{:S(2)}) async-start(bf16[8,4,512]{2,1,0:T(4,128)(2,1)} %constant_dynamic-update-slice_fusion.32), calls=%async_computation.4 | async-start | bytes 65536 | tf_op jit(solution)/shard_map/all_to_all | solution.py:39
  498.3 8.9 %all-to-all-start.10 = ((bf16[8,4,512]{2,1,0:T(4,128)(2,1)}), bf16[8,4,512]{2,1,0:T(4,128)(2,1)S(1)}, u32[]{:S(2)}, u32[]{:S(2)}) async-start(bf16[8,4,512]{2,1,0:T(4,128)(2,1)} %constant_dynamic-update-slice_fusion.82), calls=%async_computation.10 | async-start | bytes 65536 | tf_op jit(solution)/shard_map/all_to_all | solution.py:39
  562.5 81.3 %copy-start.3 = (bf16[512,1024]{1,0:T(8,128)(2,1)S(1)}, bf16[512,1024]{1,0:T(8,128)(2,1)}, u32[]{:S(2)}) copy-start(bf16[512,1024]{1,0:T(8,128)(2,1)} %param.44) | copy-start | bytes 3145732
  599.9 39.6 %all-to-all-start.5 = ((bf16[8,4,512]{2,1,0:T(4,128)(2,1)}), bf16[8,4,512]{2,1,0:T(4,128)(2,1)S(1)}, u32[]{:S(2)}, u32[]{:S(2)}) async-start(bf16[8,4,512]{2,1,0:T(4,128)(2,1)} %constant_dynamic-update-slice_fusion.42), calls=%async_computation.5 | async-start | bytes 65536 | tf_op jit(solution)/shard_map/all_to_all | solution.py:39
  639.5 9.1 %all-to-all-start.11 = ((bf16[8,4,512]{2,1,0:T(4,128)(2,1)}), bf16[8,4,512]{2,1,0:T(4,128)(2,1)S(1)}, u32[]{:S(2)}, u32[]{:S(2)}) async-start(bf16[8,4,512]{2,1,0:T(4,128)(2,1)} %constant_dynamic-update-slice_fusion.90), calls=%async_computation.11 | async-start | bytes 65536 | tf_op jit(solution)/shard_map/all_to_all | solution.py:39
  643.7 57.8 %all-reduce.25.cloned.1.call-start = ((), (), s32[]{:S(2)}) async-start(), calls=%async_computation.12 | async-start | bytes 524288
  (10 other events, 263.0 us)
Sparse Core Ops, SparseCore 0:
  73.0 54.0 all-reduce.32
  185.1 53.3 all-reduce.30
  291.5 54.3 all-reduce.28
  404.0 53.0 all-reduce.26
  649.7 51.7 all-reduce.24
